TPU v7x, 32 devices: a 4x4x1 block of a 4x4x4 slice. The times are simulated.
32 devices in a mesh: dp: 2 (over z, core), ep: 16 (over x, y).
Axes of the slice: x: 4, y: 4, z: 1, core: 2. Of those that a mesh axis runs over, the one named last changes fastest.
The devices are a block of a 4x4x4 slice.
Arguments:
- x: bfloat16 [2, 16, 256, 3584], P('dp', 'ep'), parts along dimension 0
- expert: int32 [2, 16, 256, 8], P('dp', 'ep'), parts along dimension 0
- slot: int32 [2, 16, 256, 8], P('dp', 'ep'), parts along dimension 0
- gate: float32 [2, 16, 256, 8], P('dp', 'ep'), parts along dimension 0
- w_gate: bfloat16 [32, 3584, 2560], P('ep')
- w_up: bfloat16 [32, 3584, 2560], P('ep')
- w_down: bfloat16 [32, 2560, 3584], P('ep')
- s_gate: bfloat16 [3584, 20480], replicated
- s_up: bfloat16 [3584, 20480], replicated
- s_down: bfloat16 [20480, 3584], replicated
Outputs:
- y: bfloat16 [2, 16, 256, 3584], P('dp', 'ep'), parts along dimension 0
There are 2 independent parts. A program takes and returns all parts, laid end to end along the dimension named above; an argument that names none is the same for every part.
All inputs are finite; a program needn't handle non-finite values.
Results may differ from a plain program's by a relative error of at most 0.009.
Values are sent between devices in bfloat16 or wider.
A program may use at most 1.5 GiB of HBM per device.

v0:
```python
import jax
import jax.numpy as jnp
from jax import lax
from jax.sharding import NamedSharding, PartitionSpec as P


def einsum(form, a, b):
    return jnp.einsum(form, a.astype(jnp.float32), b.astype(jnp.float32))


def for_all(x, s_gate, s_up, s_down):
    h = jax.nn.silu(einsum("...d,df->...f", x, s_gate)) * einsum("...d,df->...f", x, s_up)
    return einsum("...f,fd->...d", h.astype(jnp.bfloat16), s_down)


def solution(mesh):
    def placed(v, *spec):
        return lax.with_sharding_constraint(v, NamedSharding(mesh, P(*spec)))

    def step(x, expert, slot, gate, w_gate, w_up, w_down, s_gate, s_up, s_down):
        experts, (tokens, top) = w_gate.shape[0], expert.shape[2:]
        slots = 5 * tokens * top // (4 * experts)
        to_expert = jax.nn.one_hot(expert, experts, dtype=jnp.bfloat16)
        to_slot = jax.nn.one_hot(slot, slots, dtype=jnp.bfloat16)
        weighted = to_expert * gate[..., None].astype(jnp.bfloat16)
        dispatch = einsum("abtke,abtkc->abtec", to_expert, to_slot).astype(jnp.bfloat16)
        combine = einsum("abtke,abtkc->abtec", weighted, to_slot).astype(jnp.bfloat16)
        z = einsum("abtec,abtd->aebcd", dispatch, x).astype(jnp.bfloat16)
        z = placed(z, "dp", None, "ep", None, None)
        z = placed(z, "dp", "ep", None, None, None)
        h = jax.nn.silu(einsum("aebcd,edf->aebcf", z, w_gate))
        h = (h * einsum("aebcd,edf->aebcf", z, w_up)).astype(jnp.bfloat16)
        out = einsum("aebcf,efd->aebcd", h, w_down).astype(jnp.bfloat16)
        out = placed(out, "dp", "ep", None, None, None)
        out = placed(out, "dp", None, "ep", None, None)
        y = einsum("abtec,aebcd->abtd", combine, out)
        return (y + for_all(x, s_gate, s_up, s_down)).astype(jnp.bfloat16)

    return step
```

profile of v0, /device:TPU:112, one launch (start us, length us, event | category | flops | bytes accessed | tf_op | source)
XLA Modules:
  0.0 823.8 jit_solution(10340750054774984505)
XLA Ops:
  0.0 0.0 copy-start
  0.0 1.0 copy.11
  1.0 0.8 copy.9
  1.8 3.5 convolution_convert_fusion.2
  5.3 0.0 copy-done
  5.3 12.5 %convolution_convert_fusion = bf16[32,80,3584]{2,1,0:T(8,128)(2,1)} fusion(bf16[256,32,80]{2,1,0:T(8,128)(2,1)} %convolution_convert_fusion.2, bf16[1,1,256,3584]{3,2,1,0:T(8,128)(2,1)S(1)} %copy-done), kind=kOutput, calls=%fused_computation.24 | convolution fusion | flops 4706795520 | bytes 21495808 | tf_op jit(solution)/abtec,abtd->aebcd/dot_general | solution.py:8
  17.7 0.0 copy-start.1
  17.7 8.1 all-to-all-start
  25.8 0.0 copy-done.1
  25.8 0.1 copy.10
  25.9 3.9 convolution_convert_fusion.1
  29.8 63.2 %convolution_bitcast_fusion.1 = f32[1,1,256,20480]{3,2,1,0:T(8,128)} fusion(bf16[3584,20480]{1,0:T(8,128)(2,1)} %param.7, bf16[1,1,256,3584]{3,2,1,0:T(8,128)(2,1)S(1)} %copy-done), kind=kOutput, calls=%fused_computation.7 | convolution fusion | flops 37580963840 | bytes 169607168 | tf_op jit(solution)/...d,df->...f/dot_general | solution.py:8
  93.0 245.1 %all-to-all-done = bf16[1,16,2,1,80,3584]{5,4,2,3,0,1:T(8,128)(2,1)} async-done(((bf16[1,16,2,1,80,3584]{5,4,2,3,0,1:T(8,128)(2,1)}), bf16[1,16,2,1,80,3584]{5,4,2,3,0,1:T(8,128)(2,1)}, u32[]{:S(2)}, u32[]{:S(2)}) %all-to-all-start) | async-done | bytes 18350112 | tf_op jit(solution)/sharding_constraint;jit(solution)/sharding_constraint | solution.py:18
  338.2 57.4 %fusion.2 = f32[2,16,80,2560]{3,2,1,0:T(8,128)} fusion(bf16[2,3584,2560]{2,1,0:T(8,128)(2,1)} %param.5, bf16[1,16,2,1,80,3584]{5,4,2,3,0,1:T(8,128)(2,1)} %all-to-all-done), kind=kOutput, calls=%fused_computation.2 | convolution fusion | flops 46976204800 | bytes 81264640 | tf_op jit(solution)/aebcd,edf->aebcf/dot_general | solution.py:8
  395.6 60.7 %fusion.7 = bf16[1,2,16,80,2560]{4,3,2,1,0:T(8,128)(2,1)} fusion(f32[2,16,80,2560]{3,2,1,0:T(8,128)} %fusion.2, bf16[2,3584,2560]{2,1,0:T(8,128)(2,1)} %param.4, bf16[1,16,2,1,80,3584]{5,4,2,3,0,1:T(8,128)(2,1)} %all-to-all-done), kind=kOutput, calls=%fused_computation.10 | convolution fusion | flops 47015526400 | bytes 94371840 | tf_op jit(solution)/aebcd,edf->aebcf/dot_general | solution.py:8
  456.3 56.1 %convert_bitcast_fusion = bf16[1,2,16,1,80,3584]{5,4,2,1,3,0:T(8,128)(2,1)} fusion(bf16[2,2560,3584]{2,1,0:T(8,128)(2,1)} %param.6, bf16[1,2,16,80,2560]{4,3,2,1,0:T(8,128)(2,1)} %fusion.7), kind=kOutput, calls=%fused_computation.20 | convolution fusion | flops 46985379840 | bytes 68157440 | tf_op jit(solution)/aebcf,efd->aebcd/dot_general | solution.py:8
  512.4 15.7 %copy.15 = bf16[1,2,16,1,80,3584]{5,4,1,3,0,2:T(8,128)(2,1)} copy(bf16[1,2,16,1,80,3584]{5,4,2,1,3,0:T(8,128)(2,1)} %convert_bitcast_fusion) | data formatting | bytes 36700160 | tf_op jit(solution)/sharding_constraint;jit(solution)/sharding_constraint | solution.py:18
  528.1 6.9 all-to-all-start.1
  535.0 63.0 %fusion.72 = bf16[256,20480]{1,0:T(8,128)(2,1)} fusion(bf16[3584,20480]{1,0:T(8,128)(2,1)} %param.8, bf16[1,1,256,3584]{3,2,1,0:T(8,128)(2,1)S(1)} %copy-done, f32[1,1,256,20480]{3,2,1,0:T(8,128)} %convolution_bitcast_fusion.1), kind=kOutput, calls=%bitcast_fusion.clone.1 | convolution fusion | flops 37612421120 | bytes 180092928 | tf_op jit(solution)/...d,df->...f/dot_general | solution.py:8
  598.1 55.6 %fusion.49 = f32[256,3584]{1,0:T(8,128)} fusion(bf16[20480,3584]{1,0:T(8,128)(2,1)} %param.9, bf16[256,20480]{1,0:T(8,128)(2,1)} %fusion.72), kind=kOutput, calls=%fused_computation.50 | convolution fusion | flops 37580963840 | bytes 160956416 | tf_op jit(solution)/...f,fd->...d/dot_general | solution.py:8
  653.7 154.7 %all-to-all-done.1 = bf16[1,2,16,1,80,3584]{5,4,1,3,0,2:T(8,128)(2,1)} async-done(((bf16[1,2,16,1,80,3584]{5,4,1,3,0,2:T(8,128)(2,1)}), bf16[1,2,16,1,80,3584]{5,4,1,3,0,2:T(8,128)(2,1)}, u32[]{:S(2)}, u32[]{:S(2)}) %all-to-all-start.1) | async-done | bytes 18350112 | tf_op jit(solution)/sharding_constraint;jit(solution)/sharding_constraint | solution.py:18
  808.4 15.3 %fusion.28 = bf16[1,1,256,3584]{3,2,1,0:T(8,128)(2,1)} fusion(f32[256,3584]{1,0:T(8,128)} %fusion.49, bf16[32,80,3584]{2,1,0:T(8,128)(2,1)} %bitcast.25, bf16[256,32,80]{2,1,0:T(8,128)(2,1)} %convolution_convert_fusion.1), kind=kOutput, calls=%fused_computation.28 | convolution fusion | flops 4699455488 | bytes 25165824 | tf_op jit(solution)/abtec,aebcd->abtd/dot_general | solution.py:8
  (1 shorter events, 0.0 us)
Async XLA Ops:
  0.0 5.3 copy-start
  17.7 8.1 copy-start.1
  17.7 320.4 %all-to-all-start = ((bf16[1,16,2,1,80,3584]{5,4,2,3,0,1:T(8,128)(2,1)}), bf16[1,16,2,1,80,3584]{5,4,2,3,0,1:T(8,128)(2,1)}, u32[]{:S(2)}, u32[]{:S(2)}) async-start(bf16[1,16,2,1,80,3584]{5,4,2,3,0,1:T(8,128)(2,1)} %bitcast.143), calls=%async_computation | async-start | bytes 36700160 | tf_op jit(solution)/sharding_constraint;jit(solution)/sharding_constraint | solution.py:18
  528.1 280.2 %all-to-all-start.1 = ((bf16[1,2,16,1,80,3584]{5,4,1,3,0,2:T(8,128)(2,1)}), bf16[1,2,16,1,80,3584]{5,4,1,3,0,2:T(8,128)(2,1)}, u32[]{:S(2)}, u32[]{:S(2)}) async-start(bf16[1,2,16,1,80,3584]{5,4,1,3,0,2:T(8,128)(2,1)} %copy.15), calls=%async_computation.1 | async-start | bytes 36700160 | tf_op jit(solution)/sharding_constraint;jit(solution)/sharding_constraint | solution.py:18
where the time goes:
time: 832 us; the launch traced here: 824 us
  waiting for transfers between devices  400 us (48%)
  matrix products  391 us (47%)
  local copies, waits for them, and re-layouts  17.6 us (2%)
  starting transfers between devices  15 us (2%)
    another operation x2, waiting for transfers between devices, placed(): return lax.with_sharding_constraint(v, NamedSharding(mesh, P(*spec)))  400 us
    dot_general x10, matrix products, einsum(): return jnp.einsum(form, a.astype(jnp.float32), b.astype(jnp.float32))  391 us
  transfers between devices with their start and end apart: 2, of which 2 were waited for; matrix products, arithmetic and copies ran while one was open for 23% of the time, Pallas kernels for 0%

commit v1 on v0

v1 whole, which is shorter than its diff:
```python
import functools
import math

import jax
import jax.numpy as jnp
from jax import lax
from jax.experimental import pallas as pl
from jax.experimental.pallas import tpu as pltpu
from jax.sharding import PartitionSpec as P

MESH = pl.DeviceIdType.MESH
F32 = jnp.float32
BF16 = jnp.bfloat16


class Plan:
    def __init__(self, n, t, d, top, experts, ff, sff, ft, col):
        self.n, self.t, self.d, self.top = n, t, d, top
        self.e2 = experts // (n * n)
        self.c = 5 * t * top // (4 * experts)
        self.stride = 1 << (self.c - 1).bit_length()
        self.dh = d // 2
        self.ft, self.col = ft, col
        self.ns, self.nf = sff // ft, ff // ft
        self.cd = n // 2
        self.q = (n // self.cd) * self.e2
        self.nr = self.q * self.nf
        self.steps = self.ns + self.nr
        self.d0 = 12 * self.ns // 40
        self.sb = 25 * self.ns // 40
        self.m = (self.sb + self.nr // 2 + 5, self.sb + self.nr + 9 * self.ns // 40)


def kernel(p, x_hbm, meta, sg, su, sd, wg, wu, wd, y_hbm, xr, zbuf, zsend, ob, ret, part,
           xv, yacc, oacc, hv, zv, cs, ps, mr, gb, ub, db,
           wsem, xsem, p1s, p1r, mts, mtr, ldsem, cpsem, p2s, p2r, zlsem, obsem, p3s, p3r, csem, p4s, p4r):
    n, cc, dh = p.n, p.c, p.dh
    dp, ep = lax.axis_index("dp"), lax.axis_index("ep")
    x, y = ep // n, ep % n
    half = (slice(0, dh), slice(dh, 2 * dh))
    ab = ((x, y), (y, x))

    def mod(v):
        return lax.rem(v + 2 * n, n)

    def at(h, a, b):
        return (dp, a * n + b if h == 0 else b * n + a)

    def place(h, c, b):
        return b if h == 0 else mod(c - b)

    def remote(src, dst, s, r, dev):
        return pltpu.make_async_remote_copy(src, dst, s, r, device_id=dev, device_id_type=MESH)

    def is_r(i):
        return (i >= p.sb) & (i < p.sb + p.nr)

    def start_w(i, which):
        slot = lax.rem(i, 2)
        routed = is_r(i)

        @pl.when((i < p.steps) & jnp.logical_not(routed))
        def _():
            j = jnp.where(i < p.sb, i, i - p.nr)
            o = pl.multiple_of(j * p.ft, p.ft)
            if which == 0:
                pltpu.make_async_copy(sg.at[:, pl.ds(o, p.ft)], gb.at[slot], wsem.at[slot, 0]).start()
                pltpu.make_async_copy(su.at[:, pl.ds(o, p.ft)], ub.at[slot], wsem.at[slot, 1]).start()
            else:
                pltpu.make_async_copy(sd.at[pl.ds(o, p.ft), :], db.at[slot], wsem.at[slot, 2]).start()

        @pl.when(routed)
        def _():
            r = i - p.sb
            e = lax.rem(r // p.nf, p.e2)
            o = pl.multiple_of(lax.rem(r, p.nf) * p.ft, p.ft)
            if which == 0:
                pltpu.make_async_copy(wg.at[e, :, pl.ds(o, p.ft)], gb.at[slot], wsem.at[slot, 0]).start()
                pltpu.make_async_copy(wu.at[e, :, pl.ds(o, p.ft)], ub.at[slot], wsem.at[slot, 1]).start()
            else:
                pltpu.make_async_copy(wd.at[e, pl.ds(o, p.ft), :], db.at[slot], wsem.at[slot, 2]).start()

    def wait_w(slot, which):
        if which == 0:
            pltpu.make_async_copy(sg.at[:, pl.ds(0, p.ft)], gb.at[slot], wsem.at[slot, 0]).wait()
            pltpu.make_async_copy(su.at[:, pl.ds(0, p.ft)], ub.at[slot], wsem.at[slot, 1]).wait()
        else:
            pltpu.make_async_copy(sd.at[pl.ds(0, p.ft), :], db.at[slot], wsem.at[slot, 2]).wait()

    def p1(h, k, sending):
        a, b = ab[h]
        frm = a if sending else mod(a - k)
        dev = at(h, mod(a + k), b)
        return (
            remote(x_hbm.at[:, half[h]], xr.at[h, frm], p1s.at[h, k - 1], p1r.at[h, k - 1], dev),
            remote(meta, mr.at[h, frm], mts.at[h, k - 1], mtr.at[h, k - 1], dev),
        )

    def p2(c, h, k, sending):
        a, b = ab[h]
        to, frm = mod(b + k), (b if sending else mod(b - k))
        return remote(
            zsend.at[c, pl.ds(to * p.e2, p.e2), :, half[h]],
            zbuf.at[:, c * n + place(h, c, frm), :, half[h]],
            p2s.at[c, h, k - 1], p2r.at[c, h, k - 1], at(h, a, to),
        )

    def p3(q, cd, h, k, sending):
        a, b = ab[h]
        c, e = (q // p.e2) * p.cd + cd, lax.rem(q, p.e2)
        to, frm = mod(b + k), (b if sending else mod(b - k))
        return remote(
            ob.at[q, cd * n + place(h, c, to), :, half[h]],
            ret.at[h, frm, c, e],
            p3s.at[c, e, h, k - 1], p3r.at[c, e, h, k - 1], at(h, a, to),
        )

    def p4(c, h):
        a, b = ab[h]
        to = mod(c - b)
        k = mod(to - a)
        return k, remote(ps.at[lax.rem(c, 2), h], part.at[h, a], p4s.at[c, h], p4r.at[h, k], at(h, to, b))

    def rows_of(h, a_src, owner, weighted):
        m = mr[h, a_src]
        out = []
        for e in range(p.e2):
            first = (owner * p.e2 + e) * p.stride
            code = (lax.broadcasted_iota(jnp.int32, (cc, p.t), 0) + first).astype(F32)
            v = jnp.zeros((cc, p.t), F32)
            for k in range(p.top):
                w = m[p.top + k : p.top + k + 1, :] if weighted else 1.0
                v = jnp.where(m[k : k + 1, :] == code, w, v)
            out.append(v.astype(BF16))
        return jnp.concatenate(out, axis=0)

    def load_x(c):
        for h in range(2):
            yield pltpu.make_async_copy(xr.at[h, mod(c - ab[h][1])], ps.at[lax.rem(c, 2), h], ldsem.at[h])

    def staged(c):
        s = lax.rem(c, 2)
        yield pltpu.make_async_copy(zv.at[s], zsend.at[c], cpsem.at[0])
        for h in range(2):
            b = ab[h][1]
            yield pltpu.make_async_copy(
                zv.at[s, pl.ds(b * p.e2, p.e2), :, half[h]],
                zbuf.at[:, c * n + place(h, c, b), :, half[h]],
                cpsem.at[1 + h],
            )

    def dispatch(c):
        s = lax.rem(c, 2)

        def one(b, _):
            for h in range(2):
                a = ab[h][0]
                owner = a * n + b if h == 0 else b * n + a
                rows = rows_of(h, mod(c - ab[h][1]), owner, False)
                for o in range(0, dh, p.col):
                    z = jnp.dot(rows, ps[s, h, :, o : o + p.col], preferred_element_type=F32).astype(BF16)
                    zv[s, pl.ds(b * p.e2, p.e2), :, h * dh + o : h * dh + o + p.col] = z.reshape(p.e2, cc, p.col)
            return 0

        lax.fori_loop(0, n, one, 0)

    def load_z(q):
        chunk, e = q // p.e2, lax.rem(q, p.e2)
        return pltpu.make_async_copy(
            zbuf.at[e, pl.ds(chunk * p.cd * n, p.cd * n)], zv.at[lax.rem(q, 2)], zlsem
        )

    def put_out(q):
        s = lax.rem(q, 2)
        e = lax.rem(q, p.e2)
        yield pltpu.make_async_copy(zv.at[s], ob.at[q], obsem.at[0])
        for cd in range(p.cd):
            c = (q // p.e2) * p.cd + cd
            for h in range(2):
                b = ab[h][1]
                yield pltpu.make_async_copy(
                    zv.at[s, cd * n + place(h, c, b), :, half[h]],
                    ret.at[h, b, c, e],
                    obsem.at[1 + cd * 2 + h],
                )

    def load_ret(c):
        for h in range(2):
            yield [
                pltpu.make_async_copy(ret.at[h, b, c], cs.at[h, pl.ds(b * p.e2, p.e2)], csem.at[h, b])
                for b in range(n)
            ]

    def combine(c):
        for h in range(2):
            a, b = ab[h]
            to = mod(c - b)
            rows = []
            for o in range(n):
                rows.append(rows_of(h, to, a * n + o if h == 0 else o * n + a, True))
            rows = jnp.concatenate(rows, axis=0)
            for o in range(0, dh, p.col):
                v = lax.dot_general(
                    rows, cs[h, :, :, o : o + p.col].reshape(n * p.e2 * cc, p.col),
                    (((0,), (0,)), ((), ())), preferred_element_type=F32,
                )

                @pl.when(to == a)
                def _():
                    yacc[:, h * dh + o : h * dh + o + p.col] += v

                @pl.when(to != a)
                def _():
                    ps[lax.rem(c, 2), h, :, o : o + p.col] = v.astype(BF16)

    def up(src, rows, slot):
        for o in range(0, p.ft, p.col):
            v = src()
            g = jnp.dot(v, gb[slot, :, o : o + p.col], preferred_element_type=F32)
            u = jnp.dot(v, ub[slot, :, o : o + p.col], preferred_element_type=F32)
            hv[:rows, o : o + p.col] = (g * jax.nn.sigmoid(g) * u).astype(BF16)

    def down(acc, rows, slot):
        for o in range(0, p.d, 2 * p.col):
            acc[:, o : o + 2 * p.col] += jnp.dot(
                hv[:rows, :], db[slot, :, o : o + 2 * p.col], preferred_element_type=F32
            )

    big = p.cd * n * cc

    barrier = pltpu.get_barrier_semaphore()
    for h in range(2):
        for k in range(1, n):
            pl.semaphore_signal(barrier, inc=1, device_id=at(h, mod(ab[h][0] + k), ab[h][1]), device_id_type=MESH)
    own = pltpu.make_async_copy(x_hbm, xv, xsem.at[0])
    own.start()
    for i in range(2):
        for which in range(2):
            start_w(jnp.int32(i), which)
    pl.semaphore_wait(barrier, 2 * (n - 1))
    for k in range(1, n):
        for h in range(2):
            for copy in p1(h, k, True):
                copy.start()
    own.wait()
    mine = [pltpu.make_async_copy(xv.at[:, half[h]], xr.at[h, ab[h][0]], xsem.at[h]) for h in range(2)]
    for h in range(2):
        mine[h].start()
        mr[h, ab[h][0]] = meta[...]
    yacc[...] = jnp.zeros_like(yacc)
    oacc[...] = jnp.zeros_like(oacc)
    for h in range(2):
        mine[h].wait()

    def body(i, _):
        slot = lax.rem(i, 2)

        @pl.when(i == p.d0 - 1)
        def _():
            for h in range(2):
                for k in range(1, n):
                    for copy in p1(h, k, False):
                        copy.wait_recv()

        @pl.when((i > p.d0) & (i <= p.d0 + n))
        def _():
            c = i - p.d0 - 1
            for copy in staged(c):
                copy.wait()
            for k in range(1, n):
                for h in range(2):
                    p2(c, h, k, True).start()

        @pl.when((i >= p.d0) & (i < p.d0 + n))
        def _():
            for copy in load_x(i - p.d0):
                copy.wait()

        @pl.when((i >= p.d0 - 1) & (i < p.d0 + n - 1))
        def _():
            for copy in load_x(i - p.d0 + 1):
                copy.start()

        @pl.when((i >= p.d0) & (i < p.d0 + n))
        def _():
            c = i - p.d0
            dispatch(c)
            for copy in staged(c):
                copy.start()

        r = i - p.sb

        @pl.when((r > p.nf) & (r <= p.nr + 1) & (lax.rem(r + p.nf, p.nf) == 1))
        def _():
            q = r // p.nf - 1
            for copy in put_out(q):
                copy.wait()
            for k in range(1, n):
                for cd in range(p.cd):
                    for h in range(2):
                        p3(q, cd, h, k, True).start()

        @pl.when((r > 0) & (r <= p.nr) & (lax.rem(r + p.nf, p.nf) == 0))
        def _():
            q = r // p.nf - 1
            s = lax.rem(q, 2)

            def move(j, _):
                o = pl.multiple_of(j * cc, cc)
                zv[s, j] = oacc[pl.ds(o, cc), :].astype(BF16)
                oacc[pl.ds(o, cc), :] = jnp.zeros((cc, p.d), F32)
                return 0

            lax.fori_loop(0, p.cd * n, move, 0)
            for copy in put_out(q):
                copy.start()

        @pl.when((r >= 0) & (r < p.nr) & (lax.rem(r + p.nf, p.nf) == 0))
        def _():
            load_z(r // p.nf).wait()

        @pl.when((r >= -1) & (r < p.nr - 1) & (lax.rem(r + p.nf, p.nf) == p.nf - 1))
        def _():
            q = (r + 1) // p.nf

            @pl.when(lax.rem(q, p.e2) == 0)
            def _():
                for cd in range(p.cd):
                    for h in range(2):
                        for k in range(1, n):
                            p2((q // p.e2) * p.cd + cd, h, k, False).wait_recv()

            load_z(q).start()

        for g in range(n // p.cd):
            m = p.m[g]

            @pl.when((i > m + 1) & (i <= m + 1 + p.cd))
            def _():
                c = g * p.cd + i - m - 2
                for h in range(2):
                    k, copy = p4(c, h)

                    @pl.when(k != 0)
                    def _():
                        copy.start()

            @pl.when((i > m) & (i <= m + p.cd))
            def _():
                c = g * p.cd + i - m - 1
                for copies in load_ret(c):
                    for copy in copies:
                        copy.wait()
                if g > 0:
                    for h in range(2):
                        k, copy = p4(c - 2, h)

                        @pl.when(k != 0)
                        def _():
                            copy.wait_send()

                combine(c)

            @pl.when((i >= m) & (i < m + p.cd))
            def _():
                cd = i - m
                for e in range(p.e2):
                    for h in range(2):
                        for k in range(1, n):
                            p3(g * p.e2 + e, cd, h, k, False).wait_recv()
                for copies in load_ret(g * p.cd + cd):
                    for copy in copies:
                        copy.start()

        routed = is_r(i)
        zslot = lax.rem(jnp.maximum(r, 0) // p.nf, 2)
        wait_w(slot, 0)

        @pl.when(jnp.logical_not(routed))
        def _():
            up(lambda: xv[...], p.t, slot)

        @pl.when(routed)
        def _():
            up(lambda: zv[zslot].reshape(big, p.d), big, slot)

        start_w(i + 2, 0)
        wait_w(slot, 1)

        @pl.when(jnp.logical_not(routed))
        def _():
            down(yacc, p.t, slot)

        @pl.when(routed)
        def _():
            down(oacc, big, slot)

        start_w(i + 2, 1)
        return 0

    lax.fori_loop(0, p.steps, body, 0)

    for h in range(2):
        for k in range(1, n):
            for copy in p1(h, k, True):
                copy.wait_send()
    for c in range(n):
        for h in range(2):
            for k in range(1, n):
                p2(c, h, k, True).wait_send()
                for e in range(p.e2):
                    p3((c // p.cd) * p.e2 + e, c % p.cd, h, k, True).wait_send()
    for c in range(n - 2, n):
        for h in range(2):
            k, copy = p4(c, h)

            @pl.when(k != 0)
            def _():
                copy.wait_send()

    def arrived(h, k):
        a, b = ab[h]
        return remote(ps.at[0, h], part.at[h, mod(a - k)], p4s.at[0, h], p4r.at[h, k], at(h, mod(a + k), b))

    def fetch(h, k):
        return pltpu.make_async_copy(part.at[h, mod(ab[h][0] - k)], ps.at[lax.rem(k, 2), h], ldsem.at[h])

    for k in range(1, n):
        for h in range(2):
            arrived(h, k).wait_recv()
            fetch(h, k).start()
        for h in range(2):
            fetch(h, k).wait()
            for o in range(0, dh, p.col):
                yacc[:, h * dh + o : h * dh + o + p.col] += ps[k % 2, h, :, o : o + p.col].astype(F32)
    xv[...] = yacc[...].astype(BF16)
    last = pltpu.make_async_copy(xv, y_hbm, xsem.at[0])
    last.start()
    last.wait()


def build(mesh, ft=512, col=256):
    members = mesh.shape["ep"]
    n = math.isqrt(members)

    def step(x, expert, slot, gate, w_gate, w_up, w_down, s_gate, s_up, s_down):
        t, d = x.shape[2:]
        top = expert.shape[3]
        local, _, ff = w_gate.shape
        p = Plan(n, t, d, top, local * members, ff, s_gate.shape[1], ft, col)
        code = jnp.where(slot < p.c, expert * p.stride + slot, -1).astype(F32)
        weight = gate.astype(BF16).astype(F32)
        meta = jnp.concatenate([code[0, 0].T, weight[0, 0].T], axis=0)
        hbm = pl.BlockSpec(memory_space=pl.ANY)
        dma = pltpu.SemaphoreType.DMA
        blocks = p.cd * n
        outs = pl.pallas_call(
            functools.partial(kernel, p),
            name="moe",
            out_shape=(
                jax.ShapeDtypeStruct((t, d), BF16),
                jax.ShapeDtypeStruct((2, n, t, p.dh), BF16),
                jax.ShapeDtypeStruct((p.e2, n * n, p.c, d), BF16),
                jax.ShapeDtypeStruct((n, n * p.e2, p.c, d), BF16),
                jax.ShapeDtypeStruct((p.q, blocks, p.c, d), BF16),
                jax.ShapeDtypeStruct((2, n, n, p.e2, p.c, p.dh), BF16),
                jax.ShapeDtypeStruct((2, n, t, p.dh), BF16),
            ),
            in_specs=[hbm, pl.BlockSpec(memory_space=pltpu.VMEM)] + [hbm] * 6,
            out_specs=(hbm,) * 7,
            scratch_shapes=[
                pltpu.VMEM((t, d), BF16),
                pltpu.VMEM((t, d), F32),
                pltpu.VMEM((blocks * p.c, d), F32),
                pltpu.VMEM((max(t, blocks * p.c), ft), BF16),
                pltpu.VMEM((2, blocks, p.c, d), BF16),
                pltpu.VMEM((2, n * p.e2, p.c, p.dh), BF16),
                pltpu.VMEM((2, 2, t, p.dh), BF16),
                pltpu.VMEM((2, n, 2 * top, t), F32),
                pltpu.VMEM((2, d, ft), BF16),
                pltpu.VMEM((2, d, ft), BF16),
                pltpu.VMEM((2, ft, d), BF16),
                dma((2, 3)),
                dma((2,)),
                dma((2, n - 1)),
                dma((2, n - 1)),
                dma((2, n - 1)),
                dma((2, n - 1)),
                dma((2,)),
                dma((3,)),
                dma((n, 2, n - 1)),
                dma((n, 2, n - 1)),
                dma,
                dma((1 + 2 * p.cd,)),
                dma((n, p.e2, 2, n - 1)),
                dma((n, p.e2, 2, n - 1)),
                dma((2, n)),
                dma((n, 2)),
                dma((2, n)),
            ],
            compiler_params=pltpu.CompilerParams(
                collective_id=0, has_side_effects=True, vmem_limit_bytes=67_000_000
            ),
        )(x[0, 0], meta, s_gate, s_up, s_down, w_gate, w_up, w_down)
        return outs[0][None, None]

    tokens = P("dp", "ep", None, None)
    return jax.shard_map(
        step,
        mesh=mesh,
        in_specs=(tokens,) * 4 + (P("ep", None, None),) * 3 + (P(None, None),) * 3,
        out_specs=tokens,
        check_vma=False,
    )


def solution(mesh):
    return build(mesh)
```

time: 832 us -> 401 us (0.48)
  the two profiles are of different devices: /device:TPU:112 before, /device:TPU:97 now
where the time goes in v1:
time: 401 us
  Pallas kernels  396 us (99%)
    pallas_call x1, Pallas kernels, step(): pl.pallas_call(functools.partial(kernel, p), name='moe', out_shape=(jax.S...  396 us

profile of v1, /device:TPU:97, one launch (start us, length us, event | category | flops | bytes accessed | tf_op | source)
XLA Modules:
  0.0 401.1 jit_solution(799691486829638499)
XLA Ops:
  0.0 0.7 convert_bitcast_fusion.1
  0.7 0.7 convert_bitcast_fusion
  1.4 0.6 pad_maximum_fusion.meta
  2.0 396.2 %moe.1 = (bf16[256,3584]{1,0:T(8,128)(2,1)}, bf16[2,4,256,1792]{3,2,1,0:T(8,128)(2,1)}, bf16[2,16,80,3584]{3,2,1,0:T(8,128)(2,1)}, bf16[4,8,80,3584]{3,2,1,0:T(8...) custom-call(bf16[256,3584]{1,0:T(8,128)(2,1)} %bitcast.12, ...), custom_call_target="tpu_custom_call" | custom-call | tf_op jit(solution)/shard_map/moe/pallas_call | solution.py:457
  398.2 2.8 copy.12

commit v2 on v1

v2 whole, which is shorter than its diff:
```python
import functools
import math

import jax
import jax.numpy as jnp
from jax import lax
from jax.experimental import pallas as pl
from jax.experimental.pallas import tpu as pltpu
from jax.sharding import PartitionSpec as P

MESH = pl.DeviceIdType.MESH
F32 = jnp.float32
BF16 = jnp.bfloat16


class Plan:
    def __init__(self, n, t, d, top, experts, ff, sff, ft, col):
        self.n, self.t, self.d, self.top = n, t, d, top
        self.e2 = experts // (n * n)
        self.c = 5 * t * top // (4 * experts)
        self.stride = 1 << (self.c - 1).bit_length()
        self.dh = d // 2
        self.ft, self.col = ft, col
        self.edge = d // 4
        self.ns, self.nf = sff // ft, ff // ft
        self.sizes = (1, 2, 1)
        self.ahead = [18, 3, 0]
        self.hop, self.d0 = 7, 10
        self.lag = [[5], [8, 9], [9]]
        self.later = [1, 6, 7]
        self.sum_lag = [2, 6, 6, 4]
        self.tune()

    def tune(self):
        e2, nf = self.e2, self.nf
        self.first = [sum(self.sizes[:g]) for g in range(len(self.sizes))]
        self.start = []
        at = 0
        for ahead in self.ahead:
            self.start.append(at + ahead)
            at += ahead + e2 * nf
        self.q = len(self.sizes) * e2
        self.steps = self.ns + self.q * nf
        self.begin = [self.start[q // e2] + q % e2 * nf for q in range(self.q)]
        self.back = [self.start[g] + e2 * nf + v for g, lags in enumerate(self.lag) for v in lags]
        self.sums = [v + 1 + w for v, w in zip(self.back, self.sum_lag)]
        self.send = [self.d0 + v for v in self.later] + [self.start[0] + e2 * nf + 1]


def among(i, steps):
    hit = i == steps[0]
    for v in steps[1:]:
        hit = hit | (i == v)
    return hit


def count(i, steps):
    total = (i >= steps[0]).astype(jnp.int32)
    for v in steps[1:]:
        total = total + (i >= v).astype(jnp.int32)
    return total


def pick(g, values):
    v = jnp.int32(values[0])
    for j in range(1, len(values)):
        v = jnp.where(g >= j, jnp.int32(values[j]), v)
    return v


def kernel(p, x_hbm, meta, sg, su, sd, wg, wu, wd, y_hbm, xr, zbuf, zsend, ob, ret,
           part, xv, yacc, oacc, hv, zv, cs, ps, pf, fr, wt, mr, gb, ub, db,
           wsem, xsem, p1s, p1r, fws, fwr, mts, mtr, ldsem, cpsem, p2s, p2r, zlsem, obsem, p3s, p3r, csem, p4s, frr, p4r):
    n, cc, dh = p.n, p.c, p.dh
    dp, ep = lax.axis_index("dp"), lax.axis_index("ep")
    x, y = ep // n, ep % n
    half = (slice(0, dh), slice(dh, 2 * dh))
    ab = ((x, y), (y, x))

    def mod(v):
        return lax.rem(v + 2 * n, n)

    def at(h, a, b):
        return (dp, a * n + b if h == 0 else b * n + a)

    def place(h, c, b):
        return b if h == 0 else mod(c - b)

    def remote(src, dst, s, r, dev):
        return pltpu.make_async_remote_copy(src, dst, s, r, device_id=dev, device_id_type=MESH)

    def kind(i):
        g = count(i, p.start) - 1
        r = i - pick(g, p.start)
        routed = (g >= 0) & (r < p.e2 * p.nf)
        passed = jnp.maximum(g, 0) * (p.e2 * p.nf)
        ended = jnp.where(g >= 0, passed + p.e2 * p.nf, 0)
        return routed, g, jnp.where(routed, r, i - ended)

    def start_w(i, which):
        slot = lax.rem(i, 2)
        routed, _, r = kind(i)

        @pl.when((i < p.steps) & jnp.logical_not(routed))
        def _():
            o = pl.multiple_of(r * p.ft, p.ft)
            if which == 0:
                pltpu.make_async_copy(sg.at[:, pl.ds(o, p.ft)], gb.at[slot], wsem.at[slot, 0]).start()
                pltpu.make_async_copy(su.at[:, pl.ds(o, p.ft)], ub.at[slot], wsem.at[slot, 1]).start()
            else:
                pltpu.make_async_copy(sd.at[pl.ds(o, p.ft), :], db.at[slot], wsem.at[slot, 2]).start()

        @pl.when(routed)
        def _():
            e = r // p.nf
            o = pl.multiple_of(lax.rem(r, p.nf) * p.ft, p.ft)
            if which == 0:
                pltpu.make_async_copy(wg.at[e, :, pl.ds(o, p.ft)], gb.at[slot], wsem.at[slot, 0]).start()
                pltpu.make_async_copy(wu.at[e, :, pl.ds(o, p.ft)], ub.at[slot], wsem.at[slot, 1]).start()
            else:
                pltpu.make_async_copy(wd.at[e, pl.ds(o, p.ft), :], db.at[slot], wsem.at[slot, 2]).start()

    def wait_w(slot, which):
        if which == 0:
            pltpu.make_async_copy(sg.at[:, pl.ds(0, p.ft)], gb.at[slot], wsem.at[slot, 0]).wait()
            pltpu.make_async_copy(su.at[:, pl.ds(0, p.ft)], ub.at[slot], wsem.at[slot, 1]).wait()
        else:
            pltpu.make_async_copy(sd.at[pl.ds(0, p.ft), :], db.at[slot], wsem.at[slot, 2]).wait()

    def p1(h, k, sending):
        a, b = ab[h]
        frm = a if sending else mod(a - k)
        return remote(x_hbm.at[:, half[h]], xr.at[h, frm], p1s.at[h, k - 1], p1r.at[h, k - 1], at(h, mod(a + k), b))

    def pass_on(h, k, sending):
        a, b = ab[h]
        frm = mod(a - k) if sending else mod(a - 2 * k)
        rows = pl.ds(0 if k == 1 else p.t // 2, p.t // 2)
        j = 0 if k == 1 else 1
        return remote(xr.at[h, frm, rows], xr.at[h, frm, rows], fws.at[h, j], fwr.at[h, j], at(h, mod(a + k), b))

    def tell(h, k, sending):
        a, b = ab[h]
        frm = a if sending else mod(a - k)
        return remote(meta, mr.at[h, frm], mts.at[h, k - 1], mtr.at[h, k - 1], at(h, mod(a + k), b))

    def p2(c, h, k, sending):
        a, b = ab[h]
        to, frm = mod(b + k), (b if sending else mod(b - k))
        return remote(
            zsend.at[c, pl.ds(to * p.e2, p.e2), :, half[h]],
            zbuf.at[:, c * n + place(h, c, frm), :, half[h]],
            p2s.at[c, h, k - 1], p2r.at[c, h, k - 1], at(h, a, to),
        )

    def p3(c, e, h, k, sending):
        a, b = ab[h]
        to, frm = mod(b + k), (b if sending else mod(b - k))
        return remote(
            ob.at[c, e, place(h, c, to), :, half[h]],
            ret.at[h, frm, c, e],
            p3s.at[c, e, h, k - 1], p3r.at[c, e, h, k - 1], at(h, a, to),
        )

    quarter = (slice(0, dh // 2), slice(dh // 2, dh))

    def away(c, h):
        a, b = ab[h]
        return mod(c - b - a)

    def halfway(c, h, v):
        a, b = ab[h]
        return remote(
            ps.at[lax.rem(c, 2), h, :, quarter[v]], fr.at[h, v], p4s.at[c, h, v], frr.at[h, v],
            at(h, mod(a + 1 - 2 * v), b),
        )

    def home(c, h, side, v):
        a, b = ab[h]
        return remote(
            ps.at[lax.rem(c, 2), h, :, quarter[v]], part.at[h, side, :, quarter[v]],
            p4s.at[c, h, v], p4r.at[h, side, v], at(h, mod(a + 1 - 2 * side), b),
        )

    def rows_of(h, a_src, owner, weighted):
        m = mr[h, a_src]
        out = []
        for e in range(p.e2):
            first = (owner * p.e2 + e) * p.stride
            code = (lax.broadcasted_iota(jnp.int32, (cc, p.t), 0) + first).astype(F32)
            v = jnp.zeros((cc, p.t), F32)
            for k in range(p.top):
                w = m[p.top + k : p.top + k + 1, :] if weighted else 1.0
                v = jnp.where(m[k : k + 1, :] == code, w, v)
            out.append(v)
        return jnp.concatenate(out, axis=0)

    def load_x(c):
        for h in range(2):
            yield pltpu.make_async_copy(xr.at[h, mod(c - ab[h][1])], ps.at[lax.rem(c, 2), h], ldsem.at[h])

    def staged(c):
        s = lax.rem(c, 2)
        yield pltpu.make_async_copy(zv.at[s], zsend.at[c], cpsem.at[0])
        for h in range(2):
            b = ab[h][1]
            yield pltpu.make_async_copy(
                zv.at[s, pl.ds(b * p.e2, p.e2), :, half[h]],
                zbuf.at[:, c * n + place(h, c, b), :, half[h]],
                cpsem.at[1 + h],
            )

    def dispatch(c):
        s = lax.rem(c, 2)

        def one(b, _):
            for h in range(2):
                a = ab[h][0]
                owner = a * n + b if h == 0 else b * n + a
                rows = rows_of(h, mod(c - ab[h][1]), owner, False).astype(BF16)
                for o in range(0, dh, p.col):
                    z = jnp.dot(rows, ps[s, h, :, o : o + p.col], preferred_element_type=F32).astype(BF16)
                    zv[s, pl.ds(b * p.e2, p.e2), :, h * dh + o : h * dh + o + p.col] = z.reshape(p.e2, cc, p.col)
            return 0

        lax.fori_loop(0, n, one, 0)

    def load_z(q):
        g, e = q // p.e2, lax.rem(q, p.e2)
        c = pick(g, p.first)
        for j in range(max(p.sizes)):
            yield j < pick(g, p.sizes), c + j, pltpu.make_async_copy(
                zbuf.at[e, pl.ds((c + j) * n, n)], zv.at[lax.rem(q, 2), pl.ds(j * n, n)], zlsem.at[j]
            )

    def put_out(q):
        s = lax.rem(q, 2)
        g, e = q // p.e2, lax.rem(q, p.e2)
        for j in range(max(p.sizes)):
            c = pick(g, p.first) + j
            copies = [pltpu.make_async_copy(zv.at[s, pl.ds(j * n, n)], ob.at[c, e], obsem.at[j, 0])]
            for h in range(2):
                b = ab[h][1]
                copies.append(
                    pltpu.make_async_copy(
                        zv.at[s, j * n + place(h, c, b), :, half[h]], ret.at[h, b, c, e], obsem.at[j, 1 + h]
                    )
                )
            yield j < pick(g, p.sizes), c, copies

    def load_ret(c):
        for h in range(2):
            for b in range(n):
                yield pltpu.make_async_copy(ret.at[h, b, c], cs.at[h, pl.ds(b * p.e2, p.e2)], csem.at[h, b])

    def combine(c):
        s = lax.rem(c, 2)
        for h in range(2):
            a, b = ab[h]
            to = mod(c - b)
            rows = [rows_of(h, to, a * n + o if h == 0 else o * n + a, True) for o in range(n)]
            wt[h] = jnp.concatenate(rows, axis=0).T.astype(BF16)

            def weighed(o, w=p.col):
                v = cs[h, :, :, o : o + w].reshape(n * p.e2 * cc, w)
                return jnp.dot(wt[h], v, preferred_element_type=F32)

            k = mod(to - a)

            @pl.when(k == 0)
            def _():
                for o in range(0, dh, p.col):
                    yacc[:, h * dh + o : h * dh + o + p.col] += weighed(o)

            @pl.when(k == n // 2)
            def _():
                for v in range(2):
                    for o in range(v * dh // 2, (v + 1) * dh // 2, p.edge):
                        ps[s, h, :, o : o + p.edge] = weighed(o, p.edge).astype(BF16)
                    halfway(c, h, v).start()

            for side in range(2):

                @pl.when(k == (1, n - 1)[side])
                def _():
                    early, late = (1 - side) * dh // 2, side * dh // 2
                    for o in range(early, early + dh // 2, p.edge):
                        ps[s, h, :, o : o + p.edge] = weighed(o, p.edge).astype(BF16)
                    home(c, h, side, 1 - side).start()
                    for o in range(late, late + dh // 2, p.edge):
                        pf[h, :, o - late : o - late + p.edge] = weighed(o, p.edge)

    def add_far(c):
        for h in range(2):
            for side in range(2):

                @pl.when(away(c, h) == (1, n - 1)[side])
                def _():
                    halfway(c, h, side).wait_recv()
                    ps[lax.rem(c, 2), h, :, quarter[side]] = (pf[h] + fr[h, side].astype(F32)).astype(BF16)
                    home(c, h, side, side).start()

    def left(c):
        for h in range(2):

            @pl.when(away(c, h) != 0)
            def _():
                for v in range(2):
                    halfway(c, h, v).wait_send()

    def up(src, rows, slot):
        part_of = min(rows, n * cc) if rows > p.t else rows
        for m in range(0, rows, part_of):
            for o in range(0, p.ft, p.col):
                v = src(m, part_of)
                g = jnp.dot(v, gb[slot, :, o : o + p.col], preferred_element_type=F32)
                u = jnp.dot(v, ub[slot, :, o : o + p.col], preferred_element_type=F32)
                hv[m : m + part_of, o : o + p.col] = (g * jax.nn.sigmoid(g) * u).astype(BF16)

    def down(acc, rows, slot):
        part_of = min(rows, n * cc) if rows > p.t else rows
        for m in range(0, rows, part_of):
            for o in range(0, p.d, 2 * p.col):
                acc[m : m + part_of, o : o + 2 * p.col] += jnp.dot(
                    hv[m : m + part_of, :], db[slot, :, o : o + 2 * p.col], preferred_element_type=F32
                )

    own = pltpu.make_async_copy(x_hbm, xv, xsem.at[0])
    own.start()
    for which in range(2):
        start_w(jnp.int32(0), which)
    barrier = pltpu.get_barrier_semaphore()
    for h in range(2):
        for k in range(1, n):
            pl.semaphore_signal(barrier, inc=1, device_id=at(h, mod(ab[h][0] + k), ab[h][1]), device_id_type=MESH)
    for h in range(2):
        mr[h, ab[h][0]] = meta[...]
    yacc[...] = jnp.zeros_like(yacc)
    pl.semaphore_wait(barrier, 2 * (n - 1))
    near = (1, n - 1)
    for k in near:
        for h in range(2):
            p1(h, k, True).start()
    for k in range(1, n):
        for h in range(2):
            tell(h, k, True).start()
    own.wait()
    for which in range(2):
        start_w(jnp.int32(1), which)
    mine = [pltpu.make_async_copy(xv.at[:, half[h]], xr.at[h, ab[h][0]], xsem.at[h]) for h in range(2)]
    for h in range(2):
        mine[h].start()

    def body(i, _):
        slot = lax.rem(i, 2)

        @pl.when((i >= p.hop) & (i <= p.d0))
        def _():
            @pl.when(i == p.hop)
            def _():
                for k in near:
                    for h in range(2):
                        p1(h, k, False).wait_recv()
                        pass_on(h, k, True).start()

            @pl.when(i == p.d0)
            def _():
                oacc[...] = jnp.zeros_like(oacc)
                for h in range(2):
                    mine[h].wait()
                    for k in near:
                        pass_on(h, k, False).wait_recv()
                    for k in range(1, n):
                        tell(h, k, False).wait_recv()
                for copy in load_x(jnp.int32(0)):
                    copy.start()

        @pl.when((i >= p.begin[0] - 1) & (i <= p.begin[-1] + p.nf))
        def _():
            @pl.when(among(i, [v + p.nf for v in p.begin]))
            def _():
                q = count(i, [v + p.nf for v in p.begin]) - 1
                s = lax.rem(q, 2)

                def move(j, _):
                    o = pl.multiple_of(j * cc, cc)
                    zv[s, j] = oacc[pl.ds(o, cc), :].astype(BF16)
                    oacc[pl.ds(o, cc), :] = jnp.zeros((cc, p.d), F32)
                    return 0

                lax.fori_loop(0, pick(q // p.e2, p.sizes) * n, move, 0)
                for live, c, copies in put_out(q):

                    @pl.when(live)
                    def _():
                        for copy in copies:
                            copy.start()

            @pl.when(among(i, p.begin))
            def _():
                for live, _, copy in load_z(count(i, p.begin) - 1):

                    @pl.when(live)
                    def _():
                        copy.wait()

            @pl.when(among(i, [v - 1 for v in p.begin]))
            def _():
                q = count(i, [v - 1 for v in p.begin]) - 1
                for live, c, copy in load_z(q):

                    @pl.when(live)
                    def _():
                        @pl.when(lax.rem(q, p.e2) == 0)
                        def _():
                            for h in range(2):
                                for k in range(1, n):
                                    p2(c, h, k, False).wait_recv()

                        copy.start()

        @pl.when((i >= p.back[0]) & (i <= p.sums[-1]))
        def _():
            @pl.when(among(i, p.sums))
            def _():
                add_far(count(i, p.sums) - 1)

            @pl.when(among(i, [v + 1 for v in p.back]))
            def _():
                c = count(i, p.back) - 1 - among(i, p.back).astype(jnp.int32)
                for copy in load_ret(c):
                    copy.wait()

                @pl.when(c >= 2)
                def _():
                    left(c - 2)

                combine(c)

            @pl.when(among(i, p.back))
            def _():
                c = count(i, p.back) - 1
                for e in range(p.e2):
                    for h in range(2):
                        for k in range(1, n):
                            p3(c, e, h, k, False).wait_recv()
                for copy in load_ret(c):
                    copy.start()

        routed, g, r = kind(i)
        q = g * p.e2 + r // p.nf
        size = pick(g, p.sizes)
        zslot = lax.rem(jnp.maximum(q, 0), 2)
        wait_w(slot, 0)

        @pl.when(jnp.logical_not(routed))
        def _():
            up(lambda m, r: xv[...], p.t, slot)

        for v in sorted(set(p.sizes)):
            big = v * n * cc

            @pl.when(routed & (size == v))
            def _():
                up(lambda m, r: zv[zslot, m // cc : (m + r) // cc].reshape(r, p.d), big, slot)

        start_w(i + 2, 0)

        @pl.when((i >= p.d0) & (i <= p.send[-1]))
        def _():
            c = i - p.d0

            @pl.when((c > 0) & (c <= n))
            def _():
                for copy in staged(c - 1):
                    copy.wait()

            @pl.when(among(i, p.send))
            def _():
                c = count(i, p.send) - 1
                for k in range(1, n):
                    for h in range(2):
                        p2(c, h, k, True).start()

            @pl.when(c < n)
            def _():
                for copy in load_x(c):
                    copy.wait()

            @pl.when(c < n - 1)
            def _():
                for copy in load_x(c + 1):
                    copy.start()

            @pl.when(c < n)
            def _():
                dispatch(c)
                for copy in staged(c):
                    copy.start()

        @pl.when(among(i, [v + p.nf for v in p.begin]))
        def _():
            q = count(i, [v + p.nf for v in p.begin]) - 1
            for live, c, copies in put_out(q):

                @pl.when(live)
                def _():
                    for copy in copies:
                        copy.wait()
                    for k in range(1, n):
                        for h in range(2):
                            p3(c, lax.rem(q, p.e2), h, k, True).start()

        wait_w(slot, 1)

        @pl.when(jnp.logical_not(routed))
        def _():
            down(yacc, p.t, slot)

        for v in sorted(set(p.sizes)):
            big = v * n * cc

            @pl.when(routed & (size == v))
            def _():
                down(oacc, big, slot)

        start_w(i + 2, 1)
        return 0

    lax.fori_loop(0, p.steps, body, 0)

    for h in range(2):
        for side in range(2):
            for v in range(2):
                home(0, h, side, v).wait_recv()
        for o in range(0, dh, p.col):
            yacc[:, h * dh + o : h * dh + o + p.col] += part[h, 0, :, o : o + p.col].astype(F32) + part[
                h, 1, :, o : o + p.col
            ].astype(F32)
    last = pltpu.make_async_copy(yacc, y_hbm, xsem.at[0])
    last.start()
    for h in range(2):
        for k in near:
            p1(h, k, True).wait_send()
            pass_on(h, k, True).wait_send()
        for k in range(1, n):
            tell(h, k, True).wait_send()
    for c in range(n):
        for h in range(2):
            for k in range(1, n):
                p2(c, h, k, True).wait_send()
                for e in range(p.e2):
                    p3(c, e, h, k, True).wait_send()
    for c in range(n - 2, n):
        left(c)
    last.wait()


def build(mesh, ft=512, col=256):
    members = mesh.shape["ep"]
    n = math.isqrt(members)

    def step(x, expert, slot, gate, w_gate, w_up, w_down, s_gate, s_up, s_down):
        t, d = x.shape[2:]
        top = expert.shape[3]
        local, _, ff = w_gate.shape
        p = Plan(n, t, d, top, local * members, ff, s_gate.shape[1], ft, col)
        code = jnp.where(slot < p.c, expert * p.stride + slot, -1).astype(F32)
        weight = gate.astype(BF16).astype(F32)
        meta = jnp.concatenate([code[0, 0].T, weight[0, 0].T], axis=0)
        hbm = pl.BlockSpec(memory_space=pl.ANY)
        dma = pltpu.SemaphoreType.DMA
        blocks = max(p.sizes) * n
        outs = pl.pallas_call(
            functools.partial(kernel, p),
            name="moe",
            out_shape=(
                jax.ShapeDtypeStruct((t, d), F32),
                jax.ShapeDtypeStruct((2, n, t, p.dh), BF16),
                jax.ShapeDtypeStruct((p.e2, n * n, p.c, d), BF16),
                jax.ShapeDtypeStruct((n, n * p.e2, p.c, d), BF16),
                jax.ShapeDtypeStruct((n, p.e2, n, p.c, d), BF16),
                jax.ShapeDtypeStruct((2, n, n, p.e2, p.c, p.dh), BF16),
            ),
            in_specs=[hbm, pl.BlockSpec(memory_space=pltpu.VMEM)] + [hbm] * 6,
            out_specs=(hbm,) * 6,
            scratch_shapes=[
                pltpu.VMEM((2, 2, t, p.dh), BF16),
                pltpu.VMEM((t, d), BF16),
                pltpu.VMEM((t, d), F32),
                pltpu.VMEM((blocks * p.c, d), F32),
                pltpu.VMEM((max(t, blocks * p.c), ft), BF16),
                pltpu.VMEM((2, max(blocks, n * p.e2), p.c, d), BF16),
                pltpu.VMEM((2, n * p.e2, p.c, p.dh), BF16),
                pltpu.VMEM((2, 2, t, p.dh), BF16),
                pltpu.VMEM((2, t, p.dh // 2), F32),
                pltpu.VMEM((2, 2, t, p.dh // 2), BF16),
                pltpu.VMEM((2, t, n * p.e2 * p.c), BF16),
                pltpu.VMEM((2, n, 2 * top, t), F32),
                pltpu.VMEM((2, d, ft), BF16),
                pltpu.VMEM((2, d, ft), BF16),
                pltpu.VMEM((2, ft, d), BF16),
                dma((2, 3)),
                dma((2,)),
                dma((2, n - 1)),
                dma((2, n - 1)),
                dma((2, 2)),
                dma((2, 2)),
                dma((2, n - 1)),
                dma((2, n - 1)),
                dma((2,)),
                dma((3,)),
                dma((n, 2, n - 1)),
                dma((n, 2, n - 1)),
                dma((max(p.sizes),)),
                dma((max(p.sizes), 3)),
                dma((n, p.e2, 2, n - 1)),
                dma((n, p.e2, 2, n - 1)),
                dma((2, n)),
                dma((n, 2, 2)),
                dma((2, 2)),
                dma((2, 2, 2)),
            ],
            compiler_params=pltpu.CompilerParams(
                collective_id=0, has_side_effects=True, vmem_limit_bytes=67_000_000
            ),
        )(x[0, 0], meta, s_gate, s_up, s_down, w_gate, w_up, w_down)
        return outs[0].astype(BF16)[None, None]

    tokens = P("dp", "ep", None, None)
    return jax.shard_map(
        step,
        mesh=mesh,
        in_specs=(tokens,) * 4 + (P("ep", None, None),) * 3 + (P(None, None),) * 3,
        out_specs=tokens,
        check_vma=False,
    )


def solution(mesh):
    return build(mesh)
```

time: 401 us -> 354 us (0.88)
  the two profiles are of different devices: /device:TPU:97 before, /device:TPU:112 now
where the time goes in v2:
time: 354 us; the launch traced here: 349 us
  Pallas kernels  343 us (97%)
  other arithmetic  5.47 us (2%)
    pallas_call x1, Pallas kernels, step(): pl.pallas_call(functools.partial(kernel, p), name='moe', out_shape=(jax.S...  343 us

profile of v2, /device:TPU:112, one launch (start us, length us, event | category | flops | bytes accessed | tf_op | source)
XLA Modules:
  0.0 348.6 jit_solution(7648349399919351057)
XLA Ops:
  0.0 0.7 convert_bitcast_fusion.2
  0.7 0.7 convert_bitcast_fusion.1
  1.4 0.6 pad_maximum_fusion.meta
  2.0 343.2 %moe.1 = (f32[256,3584]{1,0:T(8,128)}, bf16[2,4,256,1792]{3,2,1,0:T(8,128)(2,1)}, bf16[2,16,80,3584]{3,2,1,0:T(8,128)(2,1)}, bf16[4,8,80,3584]{3,2,1,0:T(8,128)(...) custom-call(bf16[256,3584]{1,0:T(8,128)(2,1)} %bitcast.12, ...), custom_call_target="tpu_custom_call" | custom-call | tf_op jit(solution)/shard_map/moe/pallas_call | solution.py:574
  345.2 3.5 convert_bitcast_fusion

commit v3 on v2

--- a/solution.py
+++ b/solution.py
@@ -24,11 +24,11 @@
         self.edge = d // 4
         self.ns, self.nf = sff // ft, ff // ft
         self.sizes = (1, 2, 1)
-        self.ahead = [18, 3, 0]
-        self.hop, self.d0 = 7, 10
+        self.ahead = [20, 3, 0]
+        self.hop, self.d0 = 7, 11
         self.lag = [[5], [8, 9], [9]]
         self.later = [1, 6, 7]
-        self.sum_lag = [2, 6, 6, 4]
+        self.sum_lag = [2, 7, 7, 4]
         self.tune()
 
     def tune(self):
@@ -68,8 +68,8 @@
     return v
 
 
-def kernel(p, x_hbm, meta, sg, su, sd, wg, wu, wd, y_hbm, xr, zbuf, zsend, ob, ret,
-           part, xv, yacc, oacc, hv, zv, cs, ps, pf, fr, wt, mr, gb, ub, db,
+def kernel(p, x_hbm, expert, place_in, gate, sg, su, sd, wg, wu, wd, y_hbm, xr, zbuf, zsend, ob, ret,
+           part, meta, xv, yacc, oacc, hv, zv, cs, ps, pf, fr, wt, mr, gb, ub, db,
            wsem, xsem, p1s, p1r, fws, fwr, mts, mtr, ldsem, cpsem, p2s, p2r, zlsem, obsem, p3s, p3r, csem, p4s, frr, p4r):
     n, cc, dh = p.n, p.c, p.dh
     dp, ep = lax.axis_index("dp"), lax.axis_index("ep")
@@ -213,17 +213,13 @@
     def dispatch(c):
         s = lax.rem(c, 2)
 
-        def one(b, _):
-            for h in range(2):
-                a = ab[h][0]
-                owner = a * n + b if h == 0 else b * n + a
-                rows = rows_of(h, mod(c - ab[h][1]), owner, False).astype(BF16)
-                for o in range(0, dh, p.col):
-                    z = jnp.dot(rows, ps[s, h, :, o : o + p.col], preferred_element_type=F32).astype(BF16)
-                    zv[s, pl.ds(b * p.e2, p.e2), :, h * dh + o : h * dh + o + p.col] = z.reshape(p.e2, cc, p.col)
-            return 0
-
-        lax.fori_loop(0, n, one, 0)
+        for h in range(2):
+            a, b = ab[h]
+            rows = [rows_of(h, mod(c - b), a * n + o if h == 0 else o * n + a, False) for o in range(n)]
+            rows = jnp.concatenate(rows, axis=0).astype(BF16)
+            for o in range(0, dh, p.col):
+                z = jnp.dot(rows, ps[s, h, :, o : o + p.col], preferred_element_type=F32).astype(BF16)
+                zv[s, : n * p.e2, :, h * dh + o : h * dh + o + p.col] = z.reshape(n * p.e2, cc, p.col)
 
     def load_z(q):
         g, e = q // p.e2, lax.rem(q, p.e2)
@@ -333,6 +329,9 @@
     for h in range(2):
         for k in range(1, n):
             pl.semaphore_signal(barrier, inc=1, device_id=at(h, mod(ab[h][0] + k), ab[h][1]), device_id_type=MESH)
+    slots = place_in[...]
+    meta[: p.top, :] = jnp.where(slots < cc, expert[...] * p.stride + slots, -1).astype(F32)
+    meta[p.top :, :] = gate[...].astype(BF16).astype(F32)
     for h in range(2):
         mr[h, ab[h][0]] = meta[...]
     yacc[...] = jnp.zeros_like(yacc)
@@ -534,10 +533,9 @@
             for v in range(2):
                 home(0, h, side, v).wait_recv()
         for o in range(0, dh, p.col):
-            yacc[:, h * dh + o : h * dh + o + p.col] += part[h, 0, :, o : o + p.col].astype(F32) + part[
-                h, 1, :, o : o + p.col
-            ].astype(F32)
-    last = pltpu.make_async_copy(yacc, y_hbm, xsem.at[0])
+            v = part[h, 0, :, o : o + p.col].astype(F32) + part[h, 1, :, o : o + p.col].astype(F32)
+            xv[:, h * dh + o : h * dh + o + p.col] = (yacc[:, h * dh + o : h * dh + o + p.col] + v).astype(BF16)
+    last = pltpu.make_async_copy(xv, y_hbm, xsem.at[0])
     last.start()
     for h in range(2):
         for k in near:
@@ -565,9 +563,6 @@
         top = expert.shape[3]
         local, _, ff = w_gate.shape
         p = Plan(n, t, d, top, local * members, ff, s_gate.shape[1], ft, col)
-        code = jnp.where(slot < p.c, expert * p.stride + slot, -1).astype(F32)
-        weight = gate.astype(BF16).astype(F32)
-        meta = jnp.concatenate([code[0, 0].T, weight[0, 0].T], axis=0)
         hbm = pl.BlockSpec(memory_space=pl.ANY)
         dma = pltpu.SemaphoreType.DMA
         blocks = max(p.sizes) * n
@@ -575,17 +570,18 @@
             functools.partial(kernel, p),
             name="moe",
             out_shape=(
-                jax.ShapeDtypeStruct((t, d), F32),
+                jax.ShapeDtypeStruct((t, d), BF16),
                 jax.ShapeDtypeStruct((2, n, t, p.dh), BF16),
                 jax.ShapeDtypeStruct((p.e2, n * n, p.c, d), BF16),
                 jax.ShapeDtypeStruct((n, n * p.e2, p.c, d), BF16),
                 jax.ShapeDtypeStruct((n, p.e2, n, p.c, d), BF16),
                 jax.ShapeDtypeStruct((2, n, n, p.e2, p.c, p.dh), BF16),
             ),
-            in_specs=[hbm, pl.BlockSpec(memory_space=pltpu.VMEM)] + [hbm] * 6,
+            in_specs=[hbm] + [pl.BlockSpec(memory_space=pltpu.VMEM)] * 3 + [hbm] * 6,
             out_specs=(hbm,) * 6,
             scratch_shapes=[
                 pltpu.VMEM((2, 2, t, p.dh), BF16),
+                pltpu.VMEM((2 * top, t), F32),
                 pltpu.VMEM((t, d), BF16),
                 pltpu.VMEM((t, d), F32),
                 pltpu.VMEM((blocks * p.c, d), F32),
@@ -624,8 +620,8 @@
             compiler_params=pltpu.CompilerParams(
                 collective_id=0, has_side_effects=True, vmem_limit_bytes=67_000_000
             ),
-        )(x[0, 0], meta, s_gate, s_up, s_down, w_gate, w_up, w_down)
-        return outs[0].astype(BF16)[None, None]
+        )(x[0, 0], expert[0, 0].T, slot[0, 0].T, gate[0, 0].T, s_gate, s_up, s_down, w_gate, w_up, w_down)
+        return outs[0][None, None]
 
     tokens = P("dp", "ep", None, None)
     return jax.shard_map(

time: 354 us -> 347 us (0.980)
  other arithmetic: 5.47 us -> 0 us
  Pallas kernels: 343 us -> 339 us
    pallas_call x1, Pallas kernels: 343 us -> 339 us  [step(): pl.pallas_call(functools.partial(kernel, p), name='moe', out_shape=(jax.S...]
where the time goes in v3:
time: 347 us; the launch traced here: 342 us
  Pallas kernels  339 us (98%)
    pallas_call x1, Pallas kernels, step(): pl.pallas_call(functools.partial(kernel, p), name='moe', out_shape=(jax.S...  339 us

profile of v3, /device:TPU:112, one launch (start us, length us, event | category | flops | bytes accessed | tf_op | source)
XLA Modules:
  0.0 341.7 jit_solution(3104328294441185776)
XLA Ops:
  0.0 338.8 %moe.1 = (bf16[256,3584]{1,0:T(8,128)(2,1)}, bf16[2,4,256,1792]{3,2,1,0:T(8,128)(2,1)}, bf16[2,16,80,3584]{3,2,1,0:T(8,128)(2,1)}, bf16[4,8,80,3584]{3,2,1,0:T(8...) custom-call(bf16[256,3584]{1,0:T(8,128)(2,1)} %bitcast.11, s32[8,256]{1,0:T(8,128)} %bitcast.13, ...), custom_call_target="tpu_custom_call" | custom-call | tf_op jit(solution)/shard_map/moe/pallas_call | solution.py:569
  338.8 2.8 copy.12

commit v4 on v3

--- a/solution.py
+++ b/solution.py
@@ -21,14 +21,14 @@
         self.stride = 1 << (self.c - 1).bit_length()
         self.dh = d // 2
         self.ft, self.col = ft, col
-        self.edge = d // 4
+        self.cut = -(-self.dh // (2 * col)) * col
         self.ns, self.nf = sff // ft, ff // ft
         self.sizes = (1, 2, 1)
         self.ahead = [20, 3, 0]
         self.hop, self.d0 = 7, 11
         self.lag = [[5], [8, 9], [9]]
         self.later = [1, 6, 7]
-        self.sum_lag = [2, 7, 7, 4]
+        self.sum_lag = [4, 8, 8, 3]
         self.tune()
 
     def tune(self):
@@ -162,7 +162,8 @@
             p3s.at[c, e, h, k - 1], p3r.at[c, e, h, k - 1], at(h, a, to),
         )
 
-    quarter = (slice(0, dh // 2), slice(dh // 2, dh))
+    quarter = (slice(0, p.cut), slice(p.cut, dh))
+    wide = (p.cut, dh - p.cut)
 
     def away(c, h):
         a, b = ab[h]
@@ -171,7 +172,7 @@
     def halfway(c, h, v):
         a, b = ab[h]
         return remote(
-            ps.at[lax.rem(c, 2), h, :, quarter[v]], fr.at[h, v], p4s.at[c, h, v], frr.at[h, v],
+            ps.at[lax.rem(c, 2), h, :, quarter[v]], fr.at[h, v, :, : wide[v]], p4s.at[c, h, v], frr.at[h, v],
             at(h, mod(a + 1 - 2 * v), b),
         )
 
@@ -255,10 +256,10 @@
             a, b = ab[h]
             to = mod(c - b)
             rows = [rows_of(h, to, a * n + o if h == 0 else o * n + a, True) for o in range(n)]
-            wt[h] = jnp.concatenate(rows, axis=0).T.astype(BF16)
-
-            def weighed(o, w=p.col):
-                v = cs[h, :, :, o : o + w].reshape(n * p.e2 * cc, w)
+            wt[h] = jnp.concatenate(rows, axis=0).astype(BF16).T
+
+            def weighed(o):
+                v = cs[h, :, :, o : o + p.col].reshape(n * p.e2 * cc, p.col)
                 return jnp.dot(wt[h], v, preferred_element_type=F32)
 
             k = mod(to - a)
@@ -271,20 +272,20 @@
             @pl.when(k == n // 2)
             def _():
                 for v in range(2):
-                    for o in range(v * dh // 2, (v + 1) * dh // 2, p.edge):
-                        ps[s, h, :, o : o + p.edge] = weighed(o, p.edge).astype(BF16)
+                    for o in range(quarter[v].start, quarter[v].stop, p.col):
+                        ps[s, h, :, o : o + p.col] = weighed(o).astype(BF16)
                     halfway(c, h, v).start()
 
             for side in range(2):
 
                 @pl.when(k == (1, n - 1)[side])
                 def _():
-                    early, late = (1 - side) * dh // 2, side * dh // 2
-                    for o in range(early, early + dh // 2, p.edge):
-                        ps[s, h, :, o : o + p.edge] = weighed(o, p.edge).astype(BF16)
+                    early, late = quarter[1 - side], quarter[side]
+                    for o in range(early.start, early.stop, p.col):
+                        ps[s, h, :, o : o + p.col] = weighed(o).astype(BF16)
                     home(c, h, side, 1 - side).start()
-                    for o in range(late, late + dh // 2, p.edge):
-                        pf[h, :, o - late : o - late + p.edge] = weighed(o, p.edge)
+                    for o in range(late.start, late.stop, p.col):
+                        pf[h, :, o - late.start : o - late.start + p.col] = weighed(o)
 
     def add_far(c):
         for h in range(2):
@@ -293,7 +294,8 @@
                 @pl.when(away(c, h) == (1, n - 1)[side])
                 def _():
                     halfway(c, h, side).wait_recv()
-                    ps[lax.rem(c, 2), h, :, quarter[side]] = (pf[h] + fr[h, side].astype(F32)).astype(BF16)
+                    v = pf[h, :, : wide[side]] + fr[h, side, :, : wide[side]].astype(F32)
+                    ps[lax.rem(c, 2), h, :, quarter[side]] = v.astype(BF16)
                     home(c, h, side, side).start()
 
     def left(c):
@@ -535,8 +537,7 @@
         for o in range(0, dh, p.col):
             v = part[h, 0, :, o : o + p.col].astype(F32) + part[h, 1, :, o : o + p.col].astype(F32)
             xv[:, h * dh + o : h * dh + o + p.col] = (yacc[:, h * dh + o : h * dh + o + p.col] + v).astype(BF16)
-    last = pltpu.make_async_copy(xv, y_hbm, xsem.at[0])
-    last.start()
+        pltpu.make_async_copy(xv.at[:, half[h]], y_hbm.at[:, half[h]], xsem.at[h]).start()
     for h in range(2):
         for k in near:
             p1(h, k, True).wait_send()
@@ -551,7 +552,8 @@
                     p3(c, e, h, k, True).wait_send()
     for c in range(n - 2, n):
         left(c)
-    last.wait()
+    for h in range(2):
+        pltpu.make_async_copy(xv.at[:, half[h]], y_hbm.at[:, half[h]], xsem.at[h]).wait()
 
 
 def build(mesh, ft=512, col=256):
@@ -589,8 +591,8 @@
                 pltpu.VMEM((2, max(blocks, n * p.e2), p.c, d), BF16),
                 pltpu.VMEM((2, n * p.e2, p.c, p.dh), BF16),
                 pltpu.VMEM((2, 2, t, p.dh), BF16),
-                pltpu.VMEM((2, t, p.dh // 2), F32),
-                pltpu.VMEM((2, 2, t, p.dh // 2), BF16),
+                pltpu.VMEM((2, t, p.cut), F32),
+                pltpu.VMEM((2, 2, t, p.cut), BF16),
                 pltpu.VMEM((2, t, n * p.e2 * p.c), BF16),
                 pltpu.VMEM((2, n, 2 * top, t), F32),
                 pltpu.VMEM((2, d, ft), BF16),

time: 347 us -> 344 us (level)
  no operation moved by 1% of the time
where the time goes in v4:
time: 344 us; the launch traced here: 342 us
  Pallas kernels  339 us (99%)
    pallas_call x1, Pallas kernels, step(): pl.pallas_call(functools.partial(kernel, p), name='moe', out_shape=(jax.S...  339 us

profile of v4, /device:TPU:112, one launch (start us, length us, event | category | flops | bytes accessed | tf_op | source)
XLA Modules:
  0.0 342.1 jit_solution(11991440556600702728)
XLA Ops:
  0.0 339.3 %moe.1 = (bf16[256,3584]{1,0:T(8,128)(2,1)}, bf16[2,4,256,1792]{3,2,1,0:T(8,128)(2,1)}, bf16[2,16,80,3584]{3,2,1,0:T(8,128)(2,1)}, bf16[4,8,80,3584]{3,2,1,0:T(8...) custom-call(bf16[256,3584]{1,0:T(8,128)(2,1)} %bitcast.11, s32[8,256]{1,0:T(8,128)} %bitcast.13, ...), custom_call_target="tpu_custom_call" | custom-call | tf_op jit(solution)/shard_map/moe/pallas_call | solution.py:571
  339.3 2.8 copy.12
